TPU v7x, 256 devices: a whole 4x4x8 slice. The times are simulated.
256 devices in a mesh: expert: 8 (over y, core), shard: 32 (over x, z).
Axes of the slice: x: 4, y: 4, z: 8, core: 2. Of those that a mesh axis runs over, the one named last changes fastest.
Arguments:
- params: float32 [3, 8, 6144, 256], P(None, 'expert', 'shard'), may hold values from -3 to 3
- grads: float32 [3, 8, 6144, 256], P(None, 'expert', 'shard')
- moment: float32 [3, 8, 6144, 256], P(None, 'expert', 'shard'), may hold values from -0.6 to 0.6
- second: float32 [3, 8, 64], P(None, 'expert'), may hold values from 0.002 to 0.2
- step: int32 [1], replicated, may hold values from 1 to 8
- block_map: int32 [256], replicated, may hold values from 0 to 63, never falling along the last dimension, each value on 1 to 8 neighbouring positions
Outputs:
- new_weights: bfloat16 [3, 8, 6144, 256], P(None, 'expert')
- new_moment: float32 [3, 8, 6144, 256], P(None, 'expert', 'shard')
- new_second: float32 [3, 8, 64], P(None, 'expert')
Inputs may be any that keep to these rules, and one draw needn't show every extreme that they name: `block_map`: every block holds at least one neuron and at most 8.
All inputs are finite; a program needn't handle non-finite values.
Results may differ from a plain program's by a relative error of at most 0.001.
Values may be sent and summed in bfloat16 or wider, within the bound.
No kernel may reach another device: no remote copies, remote signals or barrier semaphores. Data moves between devices by JAX's collectives and lax.ppermute only.
A program may use at most 64 MiB of HBM per device.

v0:
```python
import math

import jax
import jax.numpy as jnp
from jax import lax
from jax.sharding import PartitionSpec as P

LEARN_RATE = 0.05
DECAY_WEIGHT = 0.1
BETA_FIRST = 0.9
BETA_SECOND = 0.95
epsilon = 1e-08


def copy_for_each(x, axis):
    length = lax.axis_size(axis)
    return lax.all_to_all(jnp.broadcast_to(x[None], (length, *x.shape)), axis, 0, 0, tiled=True)


def taken_together(x, axis):
    everything = copy_for_each(x, axis)
    return jnp.sum(everything, axis=0)


def body(params, grads, moment, second, step, block_map):
    blocks = second.shape[2]
    member_table = (block_map[:, None] == jnp.arange(blocks, dtype=jnp.int32)[None, :]).astype(
        jnp.float32
    )
    members = jnp.sum(member_table, axis=0)
    width = grads.shape[2] * lax.axis_size("shard")
    squares = jnp.sum(grads * grads, axis=2)
    local_sums = jnp.einsum("ken,nb->keb", squares, member_table, precision=lax.Precision.HIGHEST)
    block_sums = taken_together(local_sums, "shard")
    total = taken_together(jnp.sum(block_sums), "expert")
    limit = math.sqrt(3 * lax.axis_size("expert") * grads.shape[1] * width * grads.shape[3])
    clip = jnp.minimum(1.0, limit / (jnp.sqrt(total) + 1e-06))
    new_second = BETA_SECOND * second + (1.0 - BETA_SECOND) * clip * clip * block_sums / (
        width * members
    )
    new_moment = BETA_FIRST * moment + (1.0 - BETA_FIRST) * clip * grads
    step_value = step[0].astype(jnp.float32)
    first_fix = 1.0 - jnp.power(jnp.float32(BETA_FIRST), step_value)
    second_fix = 1.0 - jnp.power(jnp.float32(BETA_SECOND), step_value)
    divisor = jnp.sqrt(new_second / second_fix) + epsilon
    by_neuron = jnp.einsum("keb,nb->ken", divisor, member_table, precision=lax.Precision.HIGHEST)
    updated = (
        params * (1.0 - LEARN_RATE * DECAY_WEIGHT)
        - LEARN_RATE * (new_moment / first_fix) / by_neuron[:, :, None, :]
    )
    new_weights = lax.all_gather(updated.astype(jnp.bfloat16), "shard", axis=2, tiled=True)
    return (new_weights, new_moment, new_second)


def solution(mesh):
    placed = (
        P(None, "expert", "shard", None),
        P(None, "expert", "shard", None),
        P(None, "expert", "shard", None),
        P(None, "expert", None),
        P(),
        P(),
    )
    return jax.shard_map(
        body,
        mesh=mesh,
        in_specs=placed,
        out_specs=(
            P(None, "expert", None, None),
            P(None, "expert", "shard", None),
            P(None, "expert", None),
        ),
        check_vma=False,
    )
```

profile of v0, /device:TPU:1, one launch (start us, length us, event | category | flops | bytes accessed | tf_op | source)
XLA Modules:
  0.0 160.5 jit_solution(13806636719966661453)
XLA Ops:
  7.2 1.1 multiply_reduce_fusion
  8.3 0.8 fusion.1
  9.1 0.1 broadcast_in_dim.4
  9.2 0.5 broadcast.38
  9.7 0.8 reduce.4
  10.5 0.7 reshape.75
  11.2 11.9 %all-to-all-start = ((f32[32,1,192]{2,1,0:T(1,128)}), f32[32,1,192]{2,1,0:T(1,128)S(1)}, u32[]{:S(2)}, u32[]{:S(2)}) async-start(f32[32,1,192]{2,1,0:T(1,128)} %reshape.75), calls=%async_computation | async-start | bytes 65536 | tf_op jit(solution)/shard_map/all_to_all | solution.py:17
  23.0 0.0 all-gather.2.cloned.1.call-start
  23.1 0.8 convert_reduce_fusion
  24.6 7.2 %all-to-all-done = f32[32,1,192]{2,1,0:T(1,128)S(1)} async-done(((f32[32,1,192]{2,1,0:T(1,128)}), f32[32,1,192]{2,1,0:T(1,128)S(1)}, u32[]{:S(2)}, u32[]{:S(2)}) %all-to-all-start) | async-done | bytes 24608 | tf_op jit(solution)/shard_map/all_to_all | solution.py:17
  31.8 0.7 reduce.5
  32.5 0.1 reshape.76
  32.6 0.7 fusion.11
  33.3 0.6 broadcast_in_dim.5
  34.0 11.0 %all_to_all.11 = f32[8,1,1]{2,1,0:T(1,128)S(1)} all-to-all(f32[8,1,1]{2,1,0:T(1,128)S(1)} %broadcast_in_dim.5), channel_id=1, replica_groups=mesh['expert'=8,'shard'=32] {'expert'}, dimensions={0} | all-to-all | bytes 64 | tf_op jit(solution)/shard_map/all_to_all | solution.py:17
  45.0 0.6 reduce_sum.47
  46.3 0.7 divide_add_fusion
  47.0 0.8 fusion
  47.8 2.5 %subtract_convert_fusion = (bf16[3,1,192,256]{3,2,1,0:T(8,128)(2,1)}, f32[3,1,192,256]{3,2,1,0:T(8,128)}) fusion(f32[3,1,192,256]{3,2,1,0:T(8,128)} %param.6, f32[3,256]{1,0:T(4,128)S(1)} %fusion, f32[]{:T(128)} %bitcast, f32[3,1,192,256]{3,2,1,0:T(8,128)} %param.7, f32[]{:T(128)S(6)} %mul_shard_map.3, f32[3,1,192,256]{3,2,1,0:T(8,128)} %param.8), kind=kLoop, calls=%fused_computation | loop fusion | flops 1327104 | bytes 2657288 | tf_op jit(solution)/shard_map/convert_element_type | solution.py:51
  50.3 0.0 all-gather.2.cloned.1.call-update
  50.3 0.6 copy.15
  50.9 94.7 %all-gather.2.cloned.1.call-done = bf16[3,1,6144,256]{3,2,1,0:T(8,128)(2,1)} async-done(((bf16[3,1,192,256]{3,2,1,0:T(8,128)(2,1)}), bf16[3,1,6144,256]{3,2,1,0:T(8,128)(2,1)}) %all-gather.2.cloned.1.call-update) | async-done | bytes 9437200 | tf_op jit(solution)/shard_map/all_gather | solution.py:51
  145.6 8.0 %copy.24 = bf16[3,1,6144,256]{3,2,1,0:T(8,128)(2,1)} copy(bf16[3,1,6144,256]{3,2,1,0:T(8,128)(2,1)} %all-gather.2.cloned.1.call-done) | data formatting | bytes 18874368
  (1 shorter events, 0.0 us)
Async XLA Ops:
  11.2 20.6 %all-to-all-start = ((f32[32,1,192]{2,1,0:T(1,128)}), f32[32,1,192]{2,1,0:T(1,128)S(1)}, u32[]{:S(2)}, u32[]{:S(2)}) async-start(f32[32,1,192]{2,1,0:T(1,128)} %reshape.75), calls=%async_computation | async-start | bytes 65536 | tf_op jit(solution)/shard_map/all_to_all | solution.py:17
  23.0 122.6 %all-gather.2.cloned.1.call-start = ((), (), s32[]{:S(2)}) async-start(), calls=%async_computation.2 | async-start | bytes 9732096 | tf_op jit(solution)/shard_map/all_gather | solution.py:51
Sparse Core Ops, SparseCore 0:
  50.5 95.1 all-gather.1
where the time goes:
time: 161 us; the launch traced here: 160 us
  waiting for transfers between devices  102 us (63%)
  between operations  15.6 us (10%)
  starting transfers between devices  11.9 us (7%)
  blocking collectives  11 us (7%)
  local copies, waits for them, and re-layouts  10.6 us (7%)
  other arithmetic  7.94 us (5%)
  matrix products  1.61 us (1%)
    all_gather x1, waiting for transfers between devices, body(): lax.all_gather(updated.astype(jnp.bfloat16), 'shard', axis=2, tiled=True)  94.7 us
    all_to_all x1, starting transfers between devices, copy_for_each(): lax.all_to_all(jnp.broadcast_to(x[None], (length, *x.shape)), axis, 0, 0,...  11.9 us
    all_to_all x1, blocking collectives, copy_for_each(): lax.all_to_all(jnp.broadcast_to(x[None], (length, *x.shape)), axis, 0, 0,...  11 us
    unnamed x4, local copies, waits for them, and re-layouts  9.39 us
    all_to_all x1, waiting for transfers between devices, copy_for_each(): lax.all_to_all(jnp.broadcast_to(x[None], (length, *x.shape)), axis, 0, 0,...  7.18 us
  transfers between devices with their start and end apart: 2, of which 2 were waited for; matrix products, arithmetic and copies ran while one was open for 1% of the time, Pallas kernels for 0%

commit v1 on v0

--- a/solution.py
+++ b/solution.py
@@ -3,13 +3,20 @@
 import jax
 import jax.numpy as jnp
 from jax import lax
+from jax.experimental import pallas as pl
+from jax.experimental.pallas import tpu as pltpu
 from jax.sharding import PartitionSpec as P
+
 
 LEARN_RATE = 0.05
 DECAY_WEIGHT = 0.1
 BETA_FIRST = 0.9
 BETA_SECOND = 0.95
 epsilon = 1e-08
+
+NX, NZ = 4, 8
+ROWS = 192
+CUT = 80
 
 
 def copy_for_each(x, axis):
@@ -20,6 +27,113 @@
 def taken_together(x, axis):
     everything = copy_for_each(x, axis)
     return jnp.sum(everything, axis=0)
+
+
+def shift(value, dx, dz):
+    pairs = [
+        (x * NZ + z, (x + dx) % NX * NZ + (z + dz) % NZ) for x in range(NX) for z in range(NZ)
+    ]
+    return lax.ppermute(value, "shard", pairs)
+
+
+def assemble(pieces, places, out):
+    def kernel(*refs):
+        *ins, _, dst, sem = refs
+        me = lax.axis_index("shard")
+        x, z = me // NZ, me % NZ
+        copies = []
+        for ref, spots in zip(ins, places):
+            for g, (dx, dz, off) in enumerate(spots):
+                source = (x + dx) % NX * NZ + (z + dz) % NZ
+                start = pl.multiple_of(source * ROWS + off, 8)
+                copies.append(
+                    pltpu.make_async_copy(
+                        ref.at[pl.ds(3 * g, 3)],
+                        dst.at[:, 0, pl.ds(start, ref.shape[1]), :],
+                        sem,
+                    )
+                )
+        for copy in copies:
+            copy.start()
+        for copy in copies:
+            copy.wait()
+
+    first = out is None
+    shape = jax.ShapeDtypeStruct((3, 1, ROWS * NX * NZ, 256), jnp.bfloat16)
+    if first:
+        def body(*refs):
+            *ins, dst, sem = refs
+            kernel(*ins, None, dst, sem)
+
+        args, aliases = list(pieces), {}
+    else:
+        body, args, aliases = kernel, [*pieces, out], {len(pieces): 0}
+    return pl.pallas_call(
+        body,
+        out_shape=shape,
+        in_specs=[pl.BlockSpec(memory_space=pl.ANY)] * len(args),
+        out_specs=pl.BlockSpec(memory_space=pl.ANY),
+        scratch_shapes=[pltpu.SemaphoreType.DMA],
+        input_output_aliases=aliases,
+        compiler_params=pltpu.CompilerParams(vmem_limit_bytes=4 * 2**20),
+        name="assemble",
+    )(*args)
+
+
+def gather(own):
+    pieces, places = [], []
+
+    def put(piece, spots):
+        pieces.append(piece)
+        places.append(spots)
+
+    half = ROWS // 2
+    low = own[:, :CUT]
+    put(own, [(0, 0, 0)])
+    up, down = {0: own}, {0: own}
+    up[1] = shift(up[0], 0, 1)
+    down[1] = shift(down[0], 0, -1)
+    xm = shift(low, 1, 0)
+    xp = shift(low, -1, 0)
+    xo = shift(low, 2, 0)
+    for k in (2, 3):
+        up[k] = shift(up[k - 1], 0, 1)
+        down[k] = shift(down[k - 1], 0, -1)
+    up4 = shift(up[3][:, :half], 0, 1)
+    down4 = shift(down[3][:, half:], 0, -1)
+    for k in (1, 2, 3):
+        put(up[k], [(0, -k, 0)])
+        put(down[k], [(0, k, 0)])
+    put(up4, [(0, 4, 0)])
+    put(down4, [(0, 4, half)])
+    put(xm, [(-1, 0, 0)])
+    put(xp, [(1, 0, 0)])
+    put(xo, [(2, 0, 0)])
+    u = d = jnp.concatenate([xm, xp, xo], axis=0)
+    xs = (-1, 1, 2)
+    for k in (1, 2, 3):
+        u = shift(u, 0, 1)
+        d = shift(d, 0, -1)
+        put(u, [(x, -k, 0) for x in xs])
+        put(d, [(x, k, 0) for x in xs])
+    u = shift(u[:, : CUT // 2], 0, 1)
+    d = shift(d[:, CUT // 2 :], 0, -1)
+    put(u, [(x, 4, 0) for x in xs])
+    put(d, [(x, 4, CUT // 2) for x in xs])
+    rest = (ROWS - CUT) // 2
+    one = jnp.concatenate([p[:, CUT:] for p in (own, up[1], down[1])], axis=0)
+    four = jnp.concatenate([up4[:, CUT:], down4], axis=1)
+    two = jnp.concatenate([*(p[:, CUT:] for p in (up[2], down[2], up[3], down[3])), four], axis=0)
+    for group, zs in ((one, (0, -1, 1)), (two, (-2, 2, -3, 3, 4))):
+        u = shift(group, 1, 0)
+        d = shift(group, -1, 0)
+        put(u, [(-1, z, CUT) for z in zs])
+        put(d, [(1, z, CUT) for z in zs])
+        u = shift(u[:, :rest], 1, 0)
+        d = shift(d[:, rest:], -1, 0)
+        put(u, [(2, z, CUT) for z in zs])
+        put(d, [(2, z, CUT + rest) for z in zs])
+    return assemble(pieces, places, None)
 
 
 def body(params, grads, moment, second, step, block_map):
@@ -48,7 +162,7 @@
         params * (1.0 - LEARN_RATE * DECAY_WEIGHT)
         - LEARN_RATE * (new_moment / first_fix) / by_neuron[:, :, None, :]
     )
-    new_weights = lax.all_gather(updated.astype(jnp.bfloat16), "shard", axis=2, tiled=True)
+    new_weights = gather(updated.astype(jnp.bfloat16)[:, 0])
     return (new_weights, new_moment, new_second)
 
 
@@ -61,6 +175,7 @@
         P(),
         P(),
     )
+
     return jax.shard_map(
         body,
         mesh=mesh,

time: 161 us -> 132 us (0.82)
  the two profiles are of different devices: /device:TPU:1 before, /device:TPU:8 now
where the time goes in v1:
time: 132 us
  waiting for transfers between devices  64.2 us (49%)
  starting transfers between devices  40.6 us (31%)
  blocking collectives  8.55 us (6%)
  other arithmetic  7.92 us (6%)
  Pallas kernels  3.6 us (3%)
  local copies, waits for them, and re-layouts  2.85 us (2%)
  between operations  2.5 us (2%)
  matrix products  1.61 us (1%)
    ppermute x27, waiting for transfers between devices, shift(): return lax.ppermute(value, 'shard', pairs)  55.8 us
    ppermute x27, starting transfers between devices, shift(): return lax.ppermute(value, 'shard', pairs)  29.3 us
    all_to_all x1, starting transfers between devices, copy_for_each(): lax.all_to_all(jnp.broadcast_to(x[None], (length, *x.shape)), axis, 0, 0,...  11.3 us
    all_to_all x1, blocking collectives, copy_for_each(): lax.all_to_all(jnp.broadcast_to(x[None], (length, *x.shape)), axis, 0, 0,...  8.55 us
    all_to_all x1, waiting for transfers between devices, copy_for_each(): lax.all_to_all(jnp.broadcast_to(x[None], (length, *x.shape)), axis, 0, 0,...  8.38 us
    pallas_call x1, Pallas kernels, assemble(): pl.pallas_call(body, out_shape=shape, in_specs=[pl.BlockSpec(memory_space...  3.6 us
  transfers between devices with their start and end apart: 28, of which 13 were waited for; matrix products, arithmetic and copies ran while one was open for 1% of the time, Pallas kernels for 0%

profile of v1, /device:TPU:8, one launch (start us, length us, event | category | flops | bytes accessed | tf_op | source)
XLA Modules:
  0.0 131.8 jit_solution(17125605135218547521)
XLA Ops:
  0.6 1.1 multiply_reduce_fusion
  1.8 0.8 fusion.6
  2.6 0.1 broadcast_in_dim.4
  2.6 0.5 broadcast.38
  3.1 0.8 reduce.4
  3.9 0.7 reshape.75
  4.6 11.3 %all-to-all-start = ((f32[32,1,192]{2,1,0:T(1,128)}), f32[32,1,192]{2,1,0:T(1,128)S(1)}, u32[]{:S(2)}, u32[]{:S(2)}) async-start(f32[32,1,192]{2,1,0:T(1,128)} %reshape.75), calls=%async_computation | async-start | bytes 65536 | tf_op jit(solution)/shard_map/all_to_all | solution.py:24
  16.0 0.8 convert_reduce_fusion
  17.5 8.4 %all-to-all-done = f32[32,1,192]{2,1,0:T(1,128)S(1)} async-done(((f32[32,1,192]{2,1,0:T(1,128)}), f32[32,1,192]{2,1,0:T(1,128)S(1)}, u32[]{:S(2)}, u32[]{:S(2)}) %all-to-all-start) | async-done | bytes 24608 | tf_op jit(solution)/shard_map/all_to_all | solution.py:24
  25.9 0.7 reduce.5
  26.6 0.1 reshape.76
  26.7 0.7 fusion.16
  27.4 0.6 broadcast_in_dim.5
  28.1 8.5 %all_to_all.11 = f32[8,1,1]{2,1,0:T(1,128)S(1)} all-to-all(f32[8,1,1]{2,1,0:T(1,128)S(1)} %broadcast_in_dim.5), channel_id=1, replica_groups=mesh['expert'=8,'shard'=32] {'expert'}, dimensions={0} | all-to-all | bytes 64 | tf_op jit(solution)/shard_map/all_to_all | solution.py:24
  36.6 0.6 reduce_sum.47
  38.0 0.7 divide_add_fusion
  38.6 0.8 fusion.5
  39.5 2.4 %fusion.4 = (f32[3,1,192,256]{3,2,1,0:T(8,128)}, bf16[3,192,256]{2,1,0:T(8,128)(2,1)S(1)}) fusion(f32[3,1,192,256]{3,2,1,0:T(8,128)} %param.7, f32[]{:T(128)S(6)} %mul_shard_map.3, f32[3,1,192,256]{3,2,1,0:T(8,128)} %param.8, f32[3,256]{1,0:T(4,128)S(1)} %fusion.5, f32[]{:T(128)} %bitcast.3, f32[3,1,192,256]{3,2,1,0:T(8,128)} %param.6), kind=kLoop, calls=%fused_computation.9 | loop fusion | flops 1327104 | bytes 2657288
  41.9 0.5 collective-permute-start.1
  42.4 1.5 %collective-permute-start = (bf16[3,192,256]{2,1,0:T(8,128)(2,1)S(1)}, bf16[3,192,256]{2,1,0:T(8,128)(2,1)S(1)}, u32[]{:S(2)}, u32[]{:S(2)}) collective-permute-start(bf16[3,192,256]{2,1,0:T(8,128)(2,1)S(1)} %get-tuple-element.15.refs_0_), channel_id=1, source_target_pairs={{0,1},{1,2},{2,3},{3,4},{4,5},{5,6},{6,7},{7,0},{8,9},{9,10},{10,1... | collective-permute-start | bytes 884744 | tf_op jit(solution)/shard_map/ppermute | solution.py:36
  43.9 0.6 collective-permute-start.8
  44.5 2.7 %collective-permute-start.9 = (bf16[3,80,256]{2,1,0:T(8,128)(2,1)S(1)}, bf16[3,80,256]{2,1,0:T(8,128)(2,1)S(1)}, u32[]{:S(2)}, u32[]{:S(2)}) collective-permute-start(bf16[3,80,256]{2,1,0:T(8,128)(2,1)S(1)} %slice.70), channel_id=1, source_target_pairs={{0,24},{1,25},{2,26},{3,27},{4,28},{5,29},{6,30},{7,31},{8,0},{9,1... | collective-permute-start | bytes 368648 | tf_op jit(solution)/shard_map/ppermute | solution.py:36
  47.2 2.8 %collective-permute-done.8.refs_9_ = bf16[3,80,256]{2,1,0:T(8,128)(2,1)S(1)} collective-permute-done((bf16[3,80,256]{2,1,0:T(8,128)(2,1)S(1)}, bf16[3,80,256]{2,1,0:T(8,128)(2,1)S(1)}, u32[]{:S(2)}, u32[]{:S(2)}) %collective-permute-start.8) | collective-permute-done | bytes 122912 | tf_op jit(solution)/shard_map/ppermute | solution.py:36
  50.1 0.5 collective-permute-done.1.refs_2_
  50.6 1.7 %collective-permute-start.3 = (bf16[3,192,256]{2,1,0:T(8,128)(2,1)S(1)}, bf16[3,192,256]{2,1,0:T(8,128)(2,1)S(1)}, u32[]{:S(2)}, u32[]{:S(2)}) collective-permute-start(bf16[3,192,256]{2,1,0:T(8,128)(2,1)S(1)} %collective-permute-done.1.refs_2_), channel_id=1, source_target_pairs={{0,7},{1,0},{2,1},{3,2},{4,3},{5,4},{6,5},{7,6},{8,15},{9,8},{10,9... | collective-permute-start | bytes 884744 | tf_op jit(solution)/shard_map/ppermute | solution.py:36
  52.3 0.3 collective-permute-start.2
  52.6 0.0 collective-permute-done.9.refs_10_
  52.7 1.0 collective-permute-done.10.refs_11_
  53.6 2.0 %collective-permute-start.12 = (bf16[9,80,256]{2,1,0:T(8,128)(2,1)S(1)}, bf16[9,80,256]{2,1,0:T(8,128)(2,1)S(1)}, u32[]{:S(2)}, u32[]{:S(2)}) collective-permute-start(bf16[9,80,256]{2,1,0:T(8,128)(2,1)S(1)} %constant_dynamic-update-slice_fusion), channel_id=1, source_target_pairs={{0,7},{1,0},{2,1},{3,2},{4,3},{5,4},{6,5},{7,6},{8,15},{9,8},{10,9... | collective-permute-start | bytes 1105928 | tf_op jit(solution)/shard_map/ppermute | solution.py:36
  55.7 0.1 collective-permute-start.11
  55.8 0.1 pad_maximum_fusion
  55.8 1.8 %collective-permute-start.20 = (bf16[9,112,256]{2,1,0:T(8,128)(2,1)S(1)}, bf16[9,112,256]{2,1,0:T(8,128)(2,1)S(1)}, u32[]{:S(2)}, u32[]{:S(2)}) collective-permute-start(bf16[9,112,256]{2,1,0:T(8,128)(2,1)S(1)} %pad_maximum_fusion), channel_id=1, source_target_pairs={{0,24},{1,25},{2,26},{3,27},{4,28},{5,29},{6,30},{7,31},{8,0},{9,1... | collective-permute-start | bytes 1548296 | tf_op jit(solution)/shard_map/ppermute | solution.py:36
  57.6 2.9 %collective-permute-done.3.refs_4_ = bf16[3,192,256]{2,1,0:T(8,128)(2,1)S(1)} collective-permute-done((bf16[3,192,256]{2,1,0:T(8,128)(2,1)S(1)}, bf16[3,192,256]{2,1,0:T(8,128)(2,1)S(1)}, u32[]{:S(2)}, u32[]{:S(2)}) %collective-permute-start.3) | collective-permute-done | bytes 294944 | tf_op jit(solution)/shard_map/ppermute | solution.py:36
  60.5 2.9 %collective-permute-start.5 = (bf16[3,192,256]{2,1,0:T(8,128)(2,1)S(1)}, bf16[3,192,256]{2,1,0:T(8,128)(2,1)S(1)}, u32[]{:S(2)}, u32[]{:S(2)}) collective-permute-start(bf16[3,192,256]{2,1,0:T(8,128)(2,1)S(1)} %collective-permute-done.3.refs_4_), channel_id=1, source_target_pairs={{0,7},{1,0},{2,1},{3,2},{4,3},{5,4},{6,5},{7,6},{8,15},{9,8},{10,9... | collective-permute-start | bytes 884744 | tf_op jit(solution)/shard_map/ppermute | solution.py:36
  63.4 0.0 collective-permute-done.2.refs_3_
  63.4 0.0 collective-permute-start.4
  63.4 9.3 %collective-permute-done.5.refs_6_ = bf16[3,192,256]{2,1,0:T(8,128)(2,1)S(1)} collective-permute-done((bf16[3,192,256]{2,1,0:T(8,128)(2,1)S(1)}, bf16[3,192,256]{2,1,0:T(8,128)(2,1)S(1)}, u32[]{:S(2)}, u32[]{:S(2)}) %collective-permute-start.5) | collective-permute-done | bytes 294944 | tf_op jit(solution)/shard_map/ppermute | solution.py:36
  72.7 3.0 %collective-permute-start.7 = (bf16[3,96,256]{2,1,0:T(8,128)(2,1)S(1)}, bf16[3,96,256]{2,1,0:T(8,128)(2,1)S(1)}, u32[]{:S(2)}, u32[]{:S(2)}) collective-permute-start(bf16[3,96,256]{2,1,0:T(8,128)(2,1)S(1)} %slice.69), channel_id=1, source_target_pairs={{0,7},{1,0},{2,1},{3,2},{4,3},{5,4},{6,5},{7,6},{8,15},{9,8},{10,9... | collective-permute-start | bytes 442376 | tf_op jit(solution)/shard_map/ppermute | solution.py:36
  75.7 0.0 collective-permute-done.4.refs_5_
  75.7 0.3 collective-permute-start.6
  76.0 6.3 %collective-permute-done.6.refs_7_ = bf16[3,96,256]{2,1,0:T(8,128)(2,1)S(1)} collective-permute-done((bf16[3,96,256]{2,1,0:T(8,128)(2,1)S(1)}, bf16[3,96,256]{2,1,0:T(8,128)(2,1)S(1)}, u32[]{:S(2)}, u32[]{:S(2)}) %collective-permute-start.6) | collective-permute-done | bytes 147488 | tf_op jit(solution)/shard_map/ppermute | solution.py:36
  82.3 1.2 collective-permute-start.24
  83.6 0.9 collective-permute-start.23
  84.5 0.0 collective-permute-done.12.refs_13_
  84.5 0.0 collective-permute-start.14
  84.5 0.0 collective-permute-done.11.refs_12_
  84.5 0.7 collective-permute-start.19
  85.2 0.0 collective-permute-done.20.refs_21_
  85.2 1.9 %collective-permute-start.13 = (bf16[9,80,256]{2,1,0:T(8,128)(2,1)S(1)}, bf16[9,80,256]{2,1,0:T(8,128)(2,1)S(1)}, u32[]{:S(2)}, u32[]{:S(2)}) collective-permute-start(bf16[9,80,256]{2,1,0:T(8,128)(2,1)S(1)} %collective-permute-done.11.refs_12_), channel_id=1, source_target_pairs={{0,1},{1,2},{2,3},{3,4},{4,5},{5,6},{6,7},{7,0},{8,9},{9,10},{10,1... | collective-permute-start | bytes 1105928 | tf_op jit(solution)/shard_map/ppermute | solution.py:36
  87.1 7.0 %collective-permute-done.14.refs_15_ = bf16[9,80,256]{2,1,0:T(8,128)(2,1)S(1)} collective-permute-done((bf16[9,80,256]{2,1,0:T(8,128)(2,1)S(1)}, bf16[9,80,256]{2,1,0:T(8,128)(2,1)S(1)}, u32[]{:S(2)}, u32[]{:S(2)}) %collective-permute-start.14) | collective-permute-done | bytes 368672 | tf_op jit(solution)/shard_map/ppermute | solution.py:36
  94.1 1.0 collective-permute-done.13.refs_14_
  95.1 2.2 %collective-permute-start.15 = (bf16[9,80,256]{2,1,0:T(8,128)(2,1)S(1)}, bf16[9,80,256]{2,1,0:T(8,128)(2,1)S(1)}, u32[]{:S(2)}, u32[]{:S(2)}) collective-permute-start(bf16[9,80,256]{2,1,0:T(8,128)(2,1)S(1)} %collective-permute-done.13.refs_14_), channel_id=1, source_target_pairs={{0,1},{1,2},{2,3},{3,4},{4,5},{5,6},{6,7},{7,0},{8,9},{9,10},{10,1... | collective-permute-start | bytes 1105928 | tf_op jit(solution)/shard_map/ppermute | solution.py:36
  97.3 4.4 %collective-permute-done.24.refs_25_ = bf16[15,112,256]{2,1,0:T(8,128)(2,1)S(1)} collective-permute-done((bf16[15,112,256]{2,1,0:T(8,128)(2,1)S(1)}, bf16[15,112,256]{2,1,0:T(8,128)(2,1)S(1)}, u32[]{:S(2)}, u32[]{:S(2)}) %collective-permute-start.24) | collective-permute-done | bytes 860192 | tf_op jit(solution)/shard_map/ppermute | solution.py:36
  101.7 1.2 collective-permute-start.22
  102.9 3.9 %collective-permute-done.23.refs_24_ = bf16[15,112,256]{2,1,0:T(8,128)(2,1)S(1)} collective-permute-done((bf16[15,112,256]{2,1,0:T(8,128)(2,1)S(1)}, bf16[15,112,256]{2,1,0:T(8,128)(2,1)S(1)}, u32[]{:S(2)}, u32[]{:S(2)}) %collective-permute-start.23) | collective-permute-done | bytes 860192 | tf_op jit(solution)/shard_map/ppermute | solution.py:36
  106.8 0.0 collective-permute-start.26
  106.8 7.1 %collective-permute-done.19.refs_20_ = bf16[9,112,256]{2,1,0:T(8,128)(2,1)S(1)} collective-permute-done((bf16[9,112,256]{2,1,0:T(8,128)(2,1)S(1)}, bf16[9,112,256]{2,1,0:T(8,128)(2,1)S(1)}, u32[]{:S(2)}, u32[]{:S(2)}) %collective-permute-start.19) | collective-permute-done | bytes 516128 | tf_op jit(solution)/shard_map/ppermute | solution.py:36
  113.9 0.2 collective-permute-start.25
  114.2 1.3 %collective-permute-start.21 = (bf16[9,56,256]{2,1,0:T(8,128)(2,1)S(1)}, bf16[9,56,256]{2,1,0:T(8,128)(2,1)S(1)}, u32[]{:S(2)}, u32[]{:S(2)}) collective-permute-start(bf16[9,56,256]{2,1,0:T(8,128)(2,1)S(1)} %slice.76), channel_id=1, source_target_pairs={{0,8},{1,9},{2,10},{3,11},{4,12},{5,13},{6,14},{7,15},{8,16},{9,17... | collective-permute-start | bytes 774152 | tf_op jit(solution)/shard_map/ppermute | solution.py:36
  115.6 0.1 collective-permute-start.18
  115.7 2.1 %collective-permute-start.17 = (bf16[9,40,256]{2,1,0:T(8,128)(2,1)S(1)}, bf16[9,40,256]{2,1,0:T(8,128)(2,1)S(1)}, u32[]{:S(2)}, u32[]{:S(2)}) collective-permute-start(bf16[9,40,256]{2,1,0:T(8,128)(2,1)S(1)} %slice.71), channel_id=1, source_target_pairs={{0,1},{1,2},{2,3},{3,4},{4,5},{5,6},{6,7},{7,0},{8,9},{9,10},{10,1... | collective-permute-start | bytes 552968 | tf_op jit(solution)/shard_map/ppermute | solution.py:36
  117.8 0.6 copy.27
  118.3 9.7 %collective-permute-done.21.refs_22_ = bf16[9,56,256]{2,1,0:T(8,128)(2,1)S(1)} collective-permute-done((bf16[9,56,256]{2,1,0:T(8,128)(2,1)S(1)}, bf16[9,56,256]{2,1,0:T(8,128)(2,1)S(1)}, u32[]{:S(2)}, u32[]{:S(2)}) %collective-permute-start.21) | collective-permute-done | bytes 258080 | tf_op jit(solution)/shard_map/ppermute | solution.py:36
  128.0 3.6 %assemble.1 = bf16[3,1,6144,256]{3,2,1,0:T(8,128)(2,1)} custom-call(bf16[3,192,256]{2,1,0:T(8,128)(2,1)S(1)} %get-tuple-element.15.refs_0_, bf16[3,192,256]{2,1,0:T(8,128)(2,1)S(1)} %collective-permute-done.refs_1_, bf16[3,192,256]{2,1,0:T(8,128)(2,1)S(1)} %collective-permute-done.1.refs_2_, bf16[3,192,256]{2,1,0:T(8,128)(2,1)S(1)} %collective-permute-done.2.refs_3_, ...), custom_call_target="tpu_custom_call" | custom-call | tf_op jit(solution)/shard_map/assemble/pallas_call | solution.py:71
  (33 shorter events, 0.3 us)
Async XLA Ops:
  4.6 21.2 %all-to-all-start = ((f32[32,1,192]{2,1,0:T(1,128)}), f32[32,1,192]{2,1,0:T(1,128)S(1)}, u32[]{:S(2)}, u32[]{:S(2)}) async-start(f32[32,1,192]{2,1,0:T(1,128)} %reshape.75), calls=%async_computation | async-start | bytes 65536 | tf_op jit(solution)/shard_map/all_to_all | solution.py:24
  41.9 8.7 %collective-permute-start.1 = (bf16[3,192,256]{2,1,0:T(8,128)(2,1)S(1)}, bf16[3,192,256]{2,1,0:T(8,128)(2,1)S(1)}, u32[]{:S(2)}, u32[]{:S(2)}) collective-permute-start(bf16[3,192,256]{2,1,0:T(8,128)(2,1)S(1)} %get-tuple-element.15.refs_0_), channel_id=1, source_target_pairs={{0,7},{1,0},{2,1},{3,2},{4,3},{5,4},{6,5},{7,6},{8,15},{9,8},{10,9... | collective-permute-start | bytes 884744 | tf_op jit(solution)/shard_map/ppermute | solution.py:36
  42.4 9.9 %collective-permute-start = (bf16[3,192,256]{2,1,0:T(8,128)(2,1)S(1)}, bf16[3,192,256]{2,1,0:T(8,128)(2,1)S(1)}, u32[]{:S(2)}, u32[]{:S(2)}) collective-permute-start(bf16[3,192,256]{2,1,0:T(8,128)(2,1)S(1)} %get-tuple-element.15.refs_0_), channel_id=1, source_target_pairs={{0,1},{1,2},{2,3},{3,4},{4,5},{5,6},{6,7},{7,0},{8,9},{9,10},{10,1... | collective-permute-start | bytes 884744 | tf_op jit(solution)/shard_map/ppermute | solution.py:36
  43.9 6.2 %collective-permute-start.8 = (bf16[3,80,256]{2,1,0:T(8,128)(2,1)S(1)}, bf16[3,80,256]{2,1,0:T(8,128)(2,1)S(1)}, u32[]{:S(2)}, u32[]{:S(2)}) collective-permute-start(bf16[3,80,256]{2,1,0:T(8,128)(2,1)S(1)} %slice.70), channel_id=1, source_target_pairs={{0,8},{1,9},{2,10},{3,11},{4,12},{5,13},{6,14},{7,15},{8,16},{9,17... | collective-permute-start | bytes 368648 | tf_op jit(solution)/shard_map/ppermute | solution.py:36
  44.5 8.1 %collective-permute-start.9 = (bf16[3,80,256]{2,1,0:T(8,128)(2,1)S(1)}, bf16[3,80,256]{2,1,0:T(8,128)(2,1)S(1)}, u32[]{:S(2)}, u32[]{:S(2)}) collective-permute-start(bf16[3,80,256]{2,1,0:T(8,128)(2,1)S(1)} %slice.70), channel_id=1, source_target_pairs={{0,24},{1,25},{2,26},{3,27},{4,28},{5,29},{6,30},{7,31},{8,0},{9,1... | collective-permute-start | bytes 368648 | tf_op jit(solution)/shard_map/ppermute | solution.py:36
  47.2 6.4 %collective-permute-start.10 = (bf16[3,80,256]{2,1,0:T(8,128)(2,1)S(1)}, bf16[3,80,256]{2,1,0:T(8,128)(2,1)S(1)}, u32[]{:S(2)}, u32[]{:S(2)}) collective-permute-start(bf16[3,80,256]{2,1,0:T(8,128)(2,1)S(1)} %slice.70), channel_id=1, source_target_pairs={{0,16},{1,17},{2,18},{3,19},{4,20},{5,21},{6,22},{7,23},{8,24},{9,... | collective-permute-start | bytes 368648 | tf_op jit(solution)/shard_map/ppermute | solution.py:36
  50.6 9.9 %collective-permute-start.3 = (bf16[3,192,256]{2,1,0:T(8,128)(2,1)S(1)}, bf16[3,192,256]{2,1,0:T(8,128)(2,1)S(1)}, u32[]{:S(2)}, u32[]{:S(2)}) collective-permute-start(bf16[3,192,256]{2,1,0:T(8,128)(2,1)S(1)} %collective-permute-done.1.refs_2_), channel_id=1, source_target_pairs={{0,7},{1,0},{2,1},{3,2},{4,3},{5,4},{6,5},{7,6},{8,15},{9,8},{10,9... | collective-permute-start | bytes 884744 | tf_op jit(solution)/shard_map/ppermute | solution.py:36
  52.3 11.1 %collective-permute-start.2 = (bf16[3,192,256]{2,1,0:T(8,128)(2,1)S(1)}, bf16[3,192,256]{2,1,0:T(8,128)(2,1)S(1)}, u32[]{:S(2)}, u32[]{:S(2)}) collective-permute-start(bf16[3,192,256]{2,1,0:T(8,128)(2,1)S(1)} %collective-permute-done.refs_1_), channel_id=1, source_target_pairs={{0,1},{1,2},{2,3},{3,4},{4,5},{5,6},{6,7},{7,0},{8,9},{9,10},{10,1... | collective-permute-start | bytes 884744 | tf_op jit(solution)/shard_map/ppermute | solution.py:36
  53.6 30.8 %collective-permute-start.12 = (bf16[9,80,256]{2,1,0:T(8,128)(2,1)S(1)}, bf16[9,80,256]{2,1,0:T(8,128)(2,1)S(1)}, u32[]{:S(2)}, u32[]{:S(2)}) collective-permute-start(bf16[9,80,256]{2,1,0:T(8,128)(2,1)S(1)} %constant_dynamic-update-slice_fusion), channel_id=1, source_target_pairs={{0,7},{1,0},{2,1},{3,2},{4,3},{5,4},{6,5},{7,6},{8,15},{9,8},{10,9... | collective-permute-start | bytes 1105928 | tf_op jit(solution)/shard_map/ppermute | solution.py:36
  55.7 28.8 %collective-permute-start.11 = (bf16[9,80,256]{2,1,0:T(8,128)(2,1)S(1)}, bf16[9,80,256]{2,1,0:T(8,128)(2,1)S(1)}, u32[]{:S(2)}, u32[]{:S(2)}) collective-permute-start(bf16[9,80,256]{2,1,0:T(8,128)(2,1)S(1)} %constant_dynamic-update-slice_fusion), channel_id=1, source_target_pairs={{0,1},{1,2},{2,3},{3,4},{4,5},{5,6},{6,7},{7,0},{8,9},{9,10},{10,1... | collective-permute-start | bytes 1105928 | tf_op jit(solution)/shard_map/ppermute | solution.py:36
  55.8 29.3 %collective-permute-start.20 = (bf16[9,112,256]{2,1,0:T(8,128)(2,1)S(1)}, bf16[9,112,256]{2,1,0:T(8,128)(2,1)S(1)}, u32[]{:S(2)}, u32[]{:S(2)}) collective-permute-start(bf16[9,112,256]{2,1,0:T(8,128)(2,1)S(1)} %pad_maximum_fusion), channel_id=1, source_target_pairs={{0,24},{1,25},{2,26},{3,27},{4,28},{5,29},{6,30},{7,31},{8,0},{9,1... | collective-permute-start | bytes 1548296 | tf_op jit(solution)/shard_map/ppermute | solution.py:36
  60.5 12.2 %collective-permute-start.5 = (bf16[3,192,256]{2,1,0:T(8,128)(2,1)S(1)}, bf16[3,192,256]{2,1,0:T(8,128)(2,1)S(1)}, u32[]{:S(2)}, u32[]{:S(2)}) collective-permute-start(bf16[3,192,256]{2,1,0:T(8,128)(2,1)S(1)} %collective-permute-done.3.refs_4_), channel_id=1, source_target_pairs={{0,7},{1,0},{2,1},{3,2},{4,3},{5,4},{6,5},{7,6},{8,15},{9,8},{10,9... | collective-permute-start | bytes 884744 | tf_op jit(solution)/shard_map/ppermute | solution.py:36
  63.4 12.3 %collective-permute-start.4 = (bf16[3,192,256]{2,1,0:T(8,128)(2,1)S(1)}, bf16[3,192,256]{2,1,0:T(8,128)(2,1)S(1)}, u32[]{:S(2)}, u32[]{:S(2)}) collective-permute-start(bf16[3,192,256]{2,1,0:T(8,128)(2,1)S(1)} %collective-permute-done.2.refs_3_), channel_id=1, source_target_pairs={{0,1},{1,2},{2,3},{3,4},{4,5},{5,6},{6,7},{7,0},{8,9},{9,10},{10,1... | collective-permute-start | bytes 884744 | tf_op jit(solution)/shard_map/ppermute | solution.py:36
  72.7 9.6 %collective-permute-start.7 = (bf16[3,96,256]{2,1,0:T(8,128)(2,1)S(1)}, bf16[3,96,256]{2,1,0:T(8,128)(2,1)S(1)}, u32[]{:S(2)}, u32[]{:S(2)}) collective-permute-start(bf16[3,96,256]{2,1,0:T(8,128)(2,1)S(1)} %slice.69), channel_id=1, source_target_pairs={{0,7},{1,0},{2,1},{3,2},{4,3},{5,4},{6,5},{7,6},{8,15},{9,8},{10,9... | collective-permute-start | bytes 442376 | tf_op jit(solution)/shard_map/ppermute | solution.py:36
  75.7 6.6 %collective-permute-start.6 = (bf16[3,96,256]{2,1,0:T(8,128)(2,1)S(1)}, bf16[3,96,256]{2,1,0:T(8,128)(2,1)S(1)}, u32[]{:S(2)}, u32[]{:S(2)}) collective-permute-start(bf16[3,96,256]{2,1,0:T(8,128)(2,1)S(1)} %slice.68), channel_id=1, source_target_pairs={{0,1},{1,2},{2,3},{3,4},{4,5},{5,6},{6,7},{7,0},{8,9},{9,10},{10,1... | collective-permute-start | bytes 442376 | tf_op jit(solution)/shard_map/ppermute | solution.py:36
  82.3 19.4 %collective-permute-start.24 = (bf16[15,112,256]{2,1,0:T(8,128)(2,1)S(1)}, bf16[15,112,256]{2,1,0:T(8,128)(2,1)S(1)}, u32[]{:S(2)}, u32[]{:S(2)}) collective-permute-start(bf16[15,112,256]{2,1,0:T(8,128)(2,1)S(1)} %maximum_dynamic-update-slice_fusion), channel_id=1, source_target_pairs={{0,24},{1,25},{2,26},{3,27},{4,28},{5,29},{6,30},{7,31},{8,0},{9,1... | collective-permute-start | bytes 2580488 | tf_op jit(solution)/shard_map/ppermute | solution.py:36
  83.6 23.2 %collective-permute-start.23 = (bf16[15,112,256]{2,1,0:T(8,128)(2,1)S(1)}, bf16[15,112,256]{2,1,0:T(8,128)(2,1)S(1)}, u32[]{:S(2)}, u32[]{:S(2)}) collective-permute-start(bf16[15,112,256]{2,1,0:T(8,128)(2,1)S(1)} %maximum_dynamic-update-slice_fusion), channel_id=1, source_target_pairs={{0,8},{1,9},{2,10},{3,11},{4,12},{5,13},{6,14},{7,15},{8,16},{9,17... | collective-permute-start | bytes 2580488 | tf_op jit(solution)/shard_map/ppermute | solution.py:36
  84.5 9.7 %collective-permute-start.14 = (bf16[9,80,256]{2,1,0:T(8,128)(2,1)S(1)}, bf16[9,80,256]{2,1,0:T(8,128)(2,1)S(1)}, u32[]{:S(2)}, u32[]{:S(2)}) collective-permute-start(bf16[9,80,256]{2,1,0:T(8,128)(2,1)S(1)} %collective-permute-done.12.refs_13_), channel_id=1, source_target_pairs={{0,7},{1,0},{2,1},{3,2},{4,3},{5,4},{6,5},{7,6},{8,15},{9,8},{10,9... | collective-permute-start | bytes 1105928 | tf_op jit(solution)/shard_map/ppermute | solution.py:36
  84.5 29.5 %collective-permute-start.19 = (bf16[9,112,256]{2,1,0:T(8,128)(2,1)S(1)}, bf16[9,112,256]{2,1,0:T(8,128)(2,1)S(1)}, u32[]{:S(2)}, u32[]{:S(2)}) collective-permute-start(bf16[9,112,256]{2,1,0:T(8,128)(2,1)S(1)} %pad_maximum_fusion), channel_id=1, source_target_pairs={{0,8},{1,9},{2,10},{3,11},{4,12},{5,13},{6,14},{7,15},{8,16},{9,17... | collective-permute-start | bytes 1548296 | tf_op jit(solution)/shard_map/ppermute | solution.py:36
  85.2 9.9 %collective-permute-start.13 = (bf16[9,80,256]{2,1,0:T(8,128)(2,1)S(1)}, bf16[9,80,256]{2,1,0:T(8,128)(2,1)S(1)}, u32[]{:S(2)}, u32[]{:S(2)}) collective-permute-start(bf16[9,80,256]{2,1,0:T(8,128)(2,1)S(1)} %collective-permute-done.11.refs_12_), channel_id=1, source_target_pairs={{0,1},{1,2},{2,3},{3,4},{4,5},{5,6},{6,7},{7,0},{8,9},{9,10},{10,1... | collective-permute-start | bytes 1105928 | tf_op jit(solution)/shard_map/ppermute | solution.py:36
  94.1 20.1 %collective-permute-start.16 = (bf16[9,80,256]{2,1,0:T(8,128)(2,1)S(1)}, bf16[9,80,256]{2,1,0:T(8,128)(2,1)S(1)}, u32[]{:S(2)}, u32[]{:S(2)}) collective-permute-start(bf16[9,80,256]{2,1,0:T(8,128)(2,1)S(1)} %collective-permute-done.14.refs_15_), channel_id=1, source_target_pairs={{0,7},{1,0},{2,1},{3,2},{4,3},{5,4},{6,5},{7,6},{8,15},{9,8},{10,9... | collective-permute-start | bytes 1105928 | tf_op jit(solution)/shard_map/ppermute | solution.py:36
  95.1 20.4 %collective-permute-start.15 = (bf16[9,80,256]{2,1,0:T(8,128)(2,1)S(1)}, bf16[9,80,256]{2,1,0:T(8,128)(2,1)S(1)}, u32[]{:S(2)}, u32[]{:S(2)}) collective-permute-start(bf16[9,80,256]{2,1,0:T(8,128)(2,1)S(1)} %collective-permute-done.13.refs_14_), channel_id=1, source_target_pairs={{0,1},{1,2},{2,3},{3,4},{4,5},{5,6},{6,7},{7,0},{8,9},{9,10},{10,1... | collective-permute-start | bytes 1105928 | tf_op jit(solution)/shard_map/ppermute | solution.py:36
  101.7 14.0 %collective-permute-start.22 = (bf16[9,56,256]{2,1,0:T(8,128)(2,1)S(1)}, bf16[9,56,256]{2,1,0:T(8,128)(2,1)S(1)}, u32[]{:S(2)}, u32[]{:S(2)}) collective-permute-start(bf16[9,56,256]{2,1,0:T(8,128)(2,1)S(1)} %slice.77), channel_id=1, source_target_pairs={{0,24},{1,25},{2,26},{3,27},{4,28},{5,29},{6,30},{7,31},{8,0},{9,1... | collective-permute-start | bytes 774152 | tf_op jit(solution)/shard_map/ppermute | solution.py:36
  106.8 21.2 %collective-permute-start.26 = (bf16[15,56,256]{2,1,0:T(8,128)(2,1)S(1)}, bf16[15,56,256]{2,1,0:T(8,128)(2,1)S(1)}, u32[]{:S(2)}, u32[]{:S(2)}) collective-permute-start(bf16[15,56,256]{2,1,0:T(8,128)(2,1)S(1)} %slice.84), channel_id=1, source_target_pairs={{0,24},{1,25},{2,26},{3,27},{4,28},{5,29},{6,30},{7,31},{8,0},{9,1... | collective-permute-start | bytes 1290248 | tf_op jit(solution)/shard_map/ppermute | solution.py:36
  113.9 14.1 %collective-permute-start.25 = (bf16[15,56,256]{2,1,0:T(8,128)(2,1)S(1)}, bf16[15,56,256]{2,1,0:T(8,128)(2,1)S(1)}, u32[]{:S(2)}, u32[]{:S(2)}) collective-permute-start(bf16[15,56,256]{2,1,0:T(8,128)(2,1)S(1)} %slice.83), channel_id=1, source_target_pairs={{0,8},{1,9},{2,10},{3,11},{4,12},{5,13},{6,14},{7,15},{8,16},{9,17... | collective-permute-start | bytes 1290248 | tf_op jit(solution)/shard_map/ppermute | solution.py:36
  114.2 13.8 %collective-permute-start.21 = (bf16[9,56,256]{2,1,0:T(8,128)(2,1)S(1)}, bf16[9,56,256]{2,1,0:T(8,128)(2,1)S(1)}, u32[]{:S(2)}, u32[]{:S(2)}) collective-permute-start(bf16[9,56,256]{2,1,0:T(8,128)(2,1)S(1)} %slice.76), channel_id=1, source_target_pairs={{0,8},{1,9},{2,10},{3,11},{4,12},{5,13},{6,14},{7,15},{8,16},{9,17... | collective-permute-start | bytes 774152 | tf_op jit(solution)/shard_map/ppermute | solution.py:36
  115.6 12.5 %collective-permute-start.18 = (bf16[9,40,256]{2,1,0:T(8,128)(2,1)S(1)}, bf16[9,40,256]{2,1,0:T(8,128)(2,1)S(1)}, u32[]{:S(2)}, u32[]{:S(2)}) collective-permute-start(bf16[9,40,256]{2,1,0:T(8,128)(2,1)S(1)} %slice.72), channel_id=1, source_target_pairs={{0,7},{1,0},{2,1},{3,2},{4,3},{5,4},{6,5},{7,6},{8,15},{9,8},{10,9... | collective-permute-start | bytes 552968 | tf_op jit(solution)/shard_map/ppermute | solution.py:36
  115.7 12.3 %collective-permute-start.17 = (bf16[9,40,256]{2,1,0:T(8,128)(2,1)S(1)}, bf16[9,40,256]{2,1,0:T(8,128)(2,1)S(1)}, u32[]{:S(2)}, u32[]{:S(2)}) collective-permute-start(bf16[9,40,256]{2,1,0:T(8,128)(2,1)S(1)} %slice.71), channel_id=1, source_target_pairs={{0,1},{1,2},{2,3},{3,4},{4,5},{5,6},{6,7},{7,0},{8,9},{9,10},{10,1... | collective-permute-start | bytes 552968 | tf_op jit(solution)/shard_map/ppermute | solution.py:36
